TPU v7x, 512 devices: a whole 4x8x8 slice. The times are simulated.
512 devices in a mesh: inst: 64 (over z, x, core), tp: 8 (over y).
Axes of the slice: x: 4, y: 8, z: 8, core: 2. Of those that a mesh axis runs over, the one named last changes fastest.
Arguments:
- queries: bfloat16 [64, 4096], P('inst', 'tp'), may hold values from -360 to 360
- slot_request: int32 [64], P('inst'), may hold values from -1 to 31, as said below
- key_cache_pages: bfloat16 [2048, 128, 1024], P('inst', None, 'tp'), may hold values from -6 to 6
- value_cache_pages: bfloat16 [2048, 128, 1024], P('inst', None, 'tp'), may hold values from -6 to 6
- page_owner: int32 [2048], P('inst'), may hold values from -1 to 31, as said below
- page_fill: int32 [2048], P('inst'), may hold values from 1 to 128
- out_weight: bfloat16 [4096, 4096], P('tp', 'inst'), may hold values from -0.09375 to 0.09375
Outputs:
- projected: bfloat16 [64, 4096], P('inst', 'tp')
Inputs may be any that keep to these rules, and one draw needn't show every extreme that they name: `slot_request`: each request id appears in exactly one slot; every other slot holds -1. `page_owner`: each entry is -1 (a free page) or a request id; every request owns at least one page.
All inputs are finite; a program needn't handle non-finite values.
Results may differ from a plain program's by a relative error of at most 0.005.
Values may be sent and summed in bfloat16 or wider, within the bound.
No kernel may reach another device: no remote copies, remote signals or barrier semaphores. Data moves between devices by JAX's collectives and lax.ppermute only.
A program may use at most 64 MiB of HBM per device.

v0:
```python
import jax
import jax.numpy as jnp
from jax import lax
from jax.sharding import PartitionSpec as P

HEAD_SIZE = 128
NEG_FILL = -1e30


def sent_to_all(x, axis):
    length = lax.axis_size(axis)
    return lax.all_to_all(jnp.broadcast_to(x[None], (length, *x.shape)), axis, 0, 0, tiled=True)


def in_order(parts, dim):
    parts = jnp.moveaxis(parts, 0, dim)
    dims = parts.shape
    return parts.reshape(*dims[:dim], dims[dim] * dims[dim + 1], *dims[dim + 2 :])


def collect(x, axis, dim):
    parts = sent_to_all(x, axis)
    return in_order(parts, dim)


def taken_together(x, axis):
    everything = sent_to_all(x, axis)
    return jnp.max(everything, axis=0)


def split_up(x, dim, length):
    before, after = (x.shape[:dim], x.shape[dim + 1 :])
    return jnp.moveaxis(x.reshape(*before, length, -1, *after), dim, 0)


def summed_on_arrival(x, axis, dim):
    parts = split_up(x, dim, lax.axis_size(axis))
    arrived = lax.all_to_all(parts, axis, split_axis=0, concat_axis=0, tiled=True)
    return arrived.sum(axis=0)


def in_one_piece(arrays, axis, dim, along):
    both = jnp.concatenate(arrays, axis=along)
    result, at, finished = (summed_on_arrival(both, axis, dim), 0, [])
    for a in arrays:
        finished.append(lax.slice_in_dim(result, at, at + a.shape[along], axis=along))
        at += a.shape[along]
    return tuple(finished)


def on_device(
    queries, slot_request, key_cache_pages, value_cache_pages, page_owner, page_fill, out_weight
):
    whole_q, whole_req = (collect(queries, "inst", 0), collect(slot_request, "inst", 0))
    n_pages, page_len, kv_width = key_cache_pages.shape
    kv_local = kv_width // HEAD_SIZE
    q_local = whole_q.shape[1] // HEAD_SIZE
    query_group = q_local // kv_local
    n_slots = whole_q.shape[0]
    n_inst = lax.axis_size("inst")
    slots_dev = n_slots // n_inst
    owner_match = (page_owner[:, None] == whole_req[None, :]) & (whole_req[None, :] >= 0)
    selected_pages = jnp.dot(
        owner_match.astype(jnp.bfloat16), whole_q, preferred_element_type=jnp.float32
    ).astype(jnp.bfloat16)
    query_portion = selected_pages.reshape(n_pages, kv_local, query_group, HEAD_SIZE)
    key_portion = key_cache_pages.reshape(n_pages, page_len, kv_local, HEAD_SIZE)
    value_portion = value_cache_pages.reshape(n_pages, page_len, kv_local, HEAD_SIZE)
    scores = jnp.einsum(
        "pkgd,ptkd->pkgt", query_portion, key_portion, preferred_element_type=jnp.float32
    ) * HEAD_SIZE ** (-0.5)
    positions = jnp.arange(page_len, dtype=jnp.int32)
    is_valid = positions[None, None, None, :] < page_fill[:, None, None, None]
    scores = jnp.where(is_valid, scores, NEG_FILL)
    page_peak = jnp.max(scores, axis=-1)
    expo_vals = jnp.exp(scores - page_peak[..., None])
    page_total = jnp.sum(expo_vals, axis=-1).reshape(n_pages, q_local)
    prob_bf = expo_vals.astype(jnp.bfloat16)
    page_out = jnp.einsum(
        "pkgt,ptkd->pkgd", prob_bf, value_portion, preferred_element_type=jnp.float32
    )
    page_out = page_out.reshape(n_pages, q_local, HEAD_SIZE)
    page_peak = page_peak.reshape(n_pages, q_local)
    chosen = owner_match[:, :, None]
    slot_peak = jnp.max(jnp.where(chosen, page_peak[:, None, :], NEG_FILL), axis=0)
    weight = jnp.exp(jnp.where(chosen, page_peak[:, None, :] - slot_peak[None], NEG_FILL))
    slot_total = jnp.sum(weight * page_total[:, None, :], axis=0)
    slot_mix = jnp.einsum("prh,phd->rhd", weight, page_out, precision=lax.Precision.HIGHEST)
    global_peak = taken_together(slot_peak, "inst")
    factor = jnp.exp(slot_peak - global_peak)
    share_mix, share_total = in_one_piece(
        ((slot_mix * factor[..., None]).reshape(n_slots, q_local * HEAD_SIZE), slot_total * factor),
        "inst",
        0,
        1,
    )
    divisor = jnp.where(share_total > 0.0, share_total, 1.0)
    attention = (
        (share_mix.reshape(slots_dev, q_local, HEAD_SIZE) / divisor[..., None])
        .reshape(slots_dev, q_local * HEAD_SIZE)
        .astype(jnp.bfloat16)
    )
    every_row = collect(attention, "inst", 0)
    column_part = jnp.dot(every_row, out_weight, preferred_element_type=jnp.float32)
    partial_value = lax.all_to_all(column_part, "inst", split_axis=0, concat_axis=1, tiled=True)
    return summed_on_arrival(partial_value, "tp", 1).astype(jnp.bfloat16)


def solution(mesh):
    return jax.shard_map(
        on_device,
        mesh=mesh,
        in_specs=(
            P("inst", "tp"),
            P("inst"),
            P("inst", None, "tp"),
            P("inst", None, "tp"),
            P("inst"),
            P("inst"),
            P("tp", "inst"),
        ),
        out_specs=P("inst", "tp"),
        check_vma=False,
    )
```

profile of v0, /device:TPU:1, one launch (start us, length us, event | category | flops | bytes accessed | tf_op | source)
XLA Modules:
  0.0 119.8 jit_solution(11090895609242776855)
XLA Ops:
  0.0 0.0 copy-start
  0.7 0.6 broadcast_in_dim.82
  1.4 0.0 copy-start.5
  1.4 15.0 %all-to-all-start = ((s32[64,1,1]{2,1,0:T(1,128)}), s32[64,1,1]{2,1,0:T(1,128)S(1)}, u32[]{:S(2)}, u32[]{:S(2)}) async-start(s32[64,1,1]{2,1,0:T(1,128)} %broadcast_in_dim.82), calls=%async_computation | async-start | bytes 65536 | tf_op jit(solution)/shard_map/all_to_all | solution.py:12
  16.3 0.0 copy-done.5
  16.3 0.0 copy-start.4
  16.3 0.1 iota_compare_fusion
  16.4 0.6 copy-done.4
  17.0 0.1 broadcast_in_dim.84
  17.1 0.5 broadcast.77
  17.6 1.0 reduce.14
  18.6 0.6 reshape.189
  19.3 6.4 %all-to-all-done = s32[64,1,1]{2,1,0:T(1,128)S(1)} async-done(((s32[64,1,1]{2,1,0:T(1,128)}), s32[64,1,1]{2,1,0:T(1,128)S(1)}, u32[]{:S(2)}, u32[]{:S(2)}) %all-to-all-start) | async-done | bytes 288 | tf_op jit(solution)/shard_map/all_to_all | solution.py:12
  25.7 0.0 copy-start.3
  25.7 4.8 %all-to-all-start.1 = ((bf16[64,2,256]{2,1,0:T(2,128)(2,1)}), bf16[64,2,256]{2,1,0:T(2,128)(2,1)S(1)}, u32[]{:S(2)}, u32[]{:S(2)}) async-start(bf16[64,2,256]{2,1,0:T(2,128)(2,1)} %reshape.189), calls=%async_computation.1 | async-start | bytes 131072 | tf_op jit(solution)/shard_map/all_to_all | solution.py:12
  30.6 0.0 copy-start.1
  30.6 1.2 %reduce.6 = s32[64]{0:T(128)S(1)} reduce(s32[64,1,1]{2,1,0:T(1,128)S(1)} %all-to-all-done, s32[]{:T(128)} %constant.6.clone.1), dimensions={1,2}, to_apply=%all_to_all.29.reduce_sub_computation | reduce | bytes 516 | tf_op jit(solution)/shard_map/all_to_all | solution.py:12
  31.8 0.0 copy-done.3
  31.8 0.1 compare_and_fusion
  31.9 8.8 %all-to-all-done.1 = bf16[64,2,256]{2,1,0:T(2,128)(2,1)S(1)} async-done(((bf16[64,2,256]{2,1,0:T(2,128)(2,1)}), bf16[64,2,256]{2,1,0:T(2,128)(2,1)S(1)}, u32[]{:S(2)}, u32[]{:S(2)}) %all-to-all-start.1) | async-done | bytes 65568 | tf_op jit(solution)/shard_map/all_to_all | solution.py:12
  40.7 0.1 reshape.190
  40.7 0.2 convolution_convert_fusion
  41.0 0.0 copy-done
  41.0 0.7 fusion.21
  41.7 0.1 copy.23
  41.8 0.1 select_reduce_fusion
  41.9 0.8 reshape.191
  42.7 4.4 %all-to-all-start.2 = ((f32[64,1,256]{2,1,0:T(1,128)}), f32[64,1,256]{2,1,0:T(1,128)S(1)}, u32[]{:S(2)}, u32[]{:S(2)}) async-start(f32[64,1,256]{2,1,0:T(1,128)} %reshape.191), calls=%async_computation.2 | async-start | bytes 131072 | tf_op jit(solution)/shard_map/all_to_all | solution.py:12
  47.1 0.0 copy-done.1
  47.1 0.4 fusion.11
  47.6 0.2 fusion.9
  47.8 0.1 copy.26
  47.8 0.1 multiply_reduce_fusion
  48.0 9.3 %all-to-all-done.2 = f32[64,1,256]{2,1,0:T(1,128)S(1)} async-done(((f32[64,1,256]{2,1,0:T(1,128)}), f32[64,1,256]{2,1,0:T(1,128)S(1)}, u32[]{:S(2)}, u32[]{:S(2)}) %all-to-all-start.2) | async-done | bytes 65568 | tf_op jit(solution)/shard_map/all_to_all | solution.py:12
  57.2 0.6 broadcast.78
  57.8 0.8 reduce.15
  58.7 0.1 reshape.192
  58.8 0.1 bitcast_reduce_fusion
  58.9 0.5 fusion.1
  59.4 0.1 copy.27
  59.5 0.2 copy.28
  59.7 15.4 %all_to_all.44 = f32[64,1,516]{2,1,0:T(1,128)S(1)} all-to-all(f32[64,1,516]{2,1,0:T(1,128)S(1)} %copy.28), channel_id=1, replica_groups=mesh['inst'=64,'tp'=8] {'inst'}, dimensions={0} | all-to-all | bytes 264192 | tf_op jit(solution)/shard_map/all_to_all | solution.py:38
  75.1 0.1 reduce_sum.40
  75.2 0.1 div.14
  75.3 0.1 broadcast_in_dim.91
  75.4 1.0 reduce.16
  76.5 14.0 %all_to_all.45 = bf16[64,2,256]{2,1,0:T(2,128)(2,1)S(1)} all-to-all(bf16[64,2,256]{2,1,0:T(2,128)(2,1)S(1)} %reshape.193), channel_id=1, replica_groups=mesh['inst'=64,'tp'=8] {'inst'}, dimensions={0} | all-to-all | bytes 131072 | tf_op jit(solution)/shard_map/all_to_all | solution.py:12
  90.5 0.0 copy-start.2
  90.5 0.1 reshape.194
  90.5 0.8 copy-done.2
  91.3 0.1 fusion.3
  91.4 13.1 %all_to_all.46 = f32[64,1,64]{2,1,0:T(1,128)S(1)} all-to-all(f32[64,1,64]{2,1,0:T(1,128)S(1)} %bitcast.36), channel_id=1, replica_groups=mesh['inst'=64,'tp'=8] {'inst'}, dimensions={0} | all-to-all | bytes 32768 | tf_op jit(solution)/shard_map/all_to_all | solution.py:105
  104.6 0.5 broadcast.76
  105.1 0.7 reduce.13
  105.8 0.1 transpose_reshape.4
  105.9 13.2 %all_to_all.47 = f32[8,1,512]{2,1,0:T(1,128)S(1)} all-to-all(f32[8,1,512]{2,1,0:T(1,128)S(1)} %transpose_reshape.4), channel_id=1, replica_groups=mesh['inst'=64,'tp'=8] {'tp'}, dimensions={0} | all-to-all | bytes 32768 | tf_op jit(solution)/shard_map/all_to_all | solution.py:38
  119.2 0.6 convert_element_type.31
  (12 shorter events, 0.2 us)
Async XLA Ops:
  0.0 41.0 %copy-start = (bf16[32,128,128]{2,1,0:T(8,128)(2,1)S(1)}, bf16[32,128,128]{2,1,0:T(8,128)(2,1)}, u32[]{:S(2)}) copy-start(bf16[32,128,128]{2,1,0:T(8,128)(2,1)} %param.9) | copy-start | bytes 3145732
  1.4 15.0 %copy-start.5 = (s32[32]{0:T(128)S(1)}, s32[32]{0:T(128)}, u32[]{:S(2)}) copy-start(s32[32]{0:T(128)} %param.12) | copy-start | bytes 388
  1.4 24.4 %all-to-all-start = ((s32[64,1,1]{2,1,0:T(1,128)}), s32[64,1,1]{2,1,0:T(1,128)S(1)}, u32[]{:S(2)}, u32[]{:S(2)}) async-start(s32[64,1,1]{2,1,0:T(1,128)} %broadcast_in_dim.82), calls=%async_computation | async-start | bytes 65536 | tf_op jit(solution)/shard_map/all_to_all | solution.py:12
  16.3 0.7 copy-start.4
  25.7 6.1 %copy-start.3 = (s32[32]{0:T(128)S(1)}, s32[32]{0:T(128)}, u32[]{:S(2)}) copy-start(s32[32]{0:T(128)} %param.11) | copy-start | bytes 388
  25.7 15.0 %all-to-all-start.1 = ((bf16[64,2,256]{2,1,0:T(2,128)(2,1)}), bf16[64,2,256]{2,1,0:T(2,128)(2,1)S(1)}, u32[]{:S(2)}, u32[]{:S(2)}) async-start(bf16[64,2,256]{2,1,0:T(2,128)(2,1)} %reshape.189), calls=%async_computation.1 | async-start | bytes 131072 | tf_op jit(solution)/shard_map/all_to_all | solution.py:12
  30.6 16.5 %copy-start.1 = (bf16[32,128,128]{2,1,0:T(8,128)(2,1)S(1)}, bf16[32,128,128]{2,1,0:T(8,128)(2,1)}, u32[]{:S(2)}) copy-start(bf16[32,128,128]{2,1,0:T(8,128)(2,1)} %param.10) | copy-start | bytes 3145732
  42.7 14.6 %all-to-all-start.2 = ((f32[64,1,256]{2,1,0:T(1,128)}), f32[64,1,256]{2,1,0:T(1,128)S(1)}, u32[]{:S(2)}, u32[]{:S(2)}) async-start(f32[64,1,256]{2,1,0:T(1,128)} %reshape.191), calls=%async_computation.2 | async-start | bytes 131072 | tf_op jit(solution)/shard_map/all_to_all | solution.py:12
  90.5 0.8 copy-start.2
where the time goes:
time: 120 us
  blocking collectives  55.8 us (46%)
  waiting for transfers between devices  24.5 us (20%)
  starting transfers between devices  24.2 us (20%)
  local copies, waits for them, and re-layouts  6.63 us (6%)
  other arithmetic  5.72 us (5%)
  matrix products  1.98 us (2%)
    all_to_all x2, blocking collectives, summed_on_arrival(): lax.all_to_all(parts, axis, split_axis=0, concat_axis=0, tiled=True)  28.6 us
    all_to_all x3, waiting for transfers between devices, sent_to_all(): lax.all_to_all(jnp.broadcast_to(x[None], (length, *x.shape)), axis, 0, 0,...  24.5 us
    all_to_all x3, starting transfers between devices, sent_to_all(): lax.all_to_all(jnp.broadcast_to(x[None], (length, *x.shape)), axis, 0, 0,...  24.2 us
    all_to_all x1, blocking collectives, sent_to_all(): lax.all_to_all(jnp.broadcast_to(x[None], (length, *x.shape)), axis, 0, 0,...  14 us
    all_to_all x1, blocking collectives, on_device(): lax.all_to_all(column_part, 'inst', split_axis=0, concat_axis=1, tiled=True)  13.1 us
    unnamed x19, local copies, waits for them, and re-layouts  3.06 us
  transfers between devices with their start and end apart: 3, of which 3 were waited for; matrix products, arithmetic and copies ran while one was open for 4% of the time, Pallas kernels for 0%

commit v1 on v0

--- a/solution.py
+++ b/solution.py
@@ -5,6 +5,13 @@
 
 HEAD_SIZE = 128
 NEG_FILL = -1e30
+
+
+def trade_parts(block, name, split, join):
+    size = lax.axis_size(name)
+    blocks = jnp.stack(jnp.split(block, size, axis=split), axis=0)
+    blocks = lax.all_to_all(blocks, name, split_axis=0, concat_axis=0)
+    return jnp.concatenate(blocks, axis=join)
 
 
 def sent_to_all(x, axis):
@@ -102,7 +109,7 @@
     )
     every_row = collect(attention, "inst", 0)
     column_part = jnp.dot(every_row, out_weight, preferred_element_type=jnp.float32)
-    partial_value = lax.all_to_all(column_part, "inst", split_axis=0, concat_axis=1, tiled=True)
+    partial_value = trade_parts(column_part, "inst", 0, 1)
     return summed_on_arrival(partial_value, "tp", 1).astype(jnp.bfloat16)
 
 

time: 120 us -> 121 us (level)
    unnamed x19 -> x82, local copies, waits for them, and re-layouts: 3.06 us -> 3.7 us
where the time goes in v1:
time: 121 us
  blocking collectives  55.8 us (46%)
  waiting for transfers between devices  24.5 us (20%)
  starting transfers between devices  24.2 us (20%)
  local copies, waits for them, and re-layouts  7.29 us (6%)
  other arithmetic  5.72 us (5%)
  matrix products  1.98 us (2%)
    all_to_all x2, blocking collectives, summed_on_arrival(): lax.all_to_all(parts, axis, split_axis=0, concat_axis=0, tiled=True)  28.6 us
    all_to_all x3, waiting for transfers between devices, sent_to_all(): lax.all_to_all(jnp.broadcast_to(x[None], (length, *x.shape)), axis, 0, 0,...  24.5 us
    all_to_all x3, starting transfers between devices, sent_to_all(): lax.all_to_all(jnp.broadcast_to(x[None], (length, *x.shape)), axis, 0, 0,...  24.2 us
    all_to_all x1, blocking collectives, sent_to_all(): lax.all_to_all(jnp.broadcast_to(x[None], (length, *x.shape)), axis, 0, 0,...  14 us
    all_to_all x1, blocking collectives, trade_parts(): blocks = lax.all_to_all(blocks, name, split_axis=0, concat_axis=0)  13.1 us
    unnamed x82, local copies, waits for them, and re-layouts  3.7 us
  transfers between devices with their start and end apart: 3, of which 3 were waited for; matrix products, arithmetic and copies ran while one was open for 4% of the time, Pallas kernels for 0%

profile of v1, /device:TPU:1, one launch (start us, length us, event | category | flops | bytes accessed | tf_op | source)
XLA Modules:
  0.0 120.6 jit_solution(10245821674199624380)
XLA Ops:
  0.0 0.0 copy-start
  0.7 0.6 broadcast_in_dim.82
  1.4 0.0 copy-start.5
  1.4 15.0 %all-to-all-start = ((s32[64,1,1]{2,1,0:T(1,128)}), s32[64,1,1]{2,1,0:T(1,128)S(1)}, u32[]{:S(2)}, u32[]{:S(2)}) async-start(s32[64,1,1]{2,1,0:T(1,128)} %broadcast_in_dim.82), calls=%async_computation | async-start | bytes 65536 | tf_op jit(solution)/shard_map/all_to_all | solution.py:19
  16.3 0.0 copy-done.5
  16.3 0.0 copy-start.4
  16.3 0.1 iota_compare_fusion
  16.4 0.6 copy-done.4
  17.0 0.1 broadcast_in_dim.84
  17.1 0.5 broadcast.77
  17.6 1.0 reduce.14
  18.6 0.6 reshape.182
  19.3 6.4 %all-to-all-done = s32[64,1,1]{2,1,0:T(1,128)S(1)} async-done(((s32[64,1,1]{2,1,0:T(1,128)}), s32[64,1,1]{2,1,0:T(1,128)S(1)}, u32[]{:S(2)}, u32[]{:S(2)}) %all-to-all-start) | async-done | bytes 288 | tf_op jit(solution)/shard_map/all_to_all | solution.py:19
  25.7 0.0 copy-start.3
  25.7 4.8 %all-to-all-start.1 = ((bf16[64,2,256]{2,1,0:T(2,128)(2,1)}), bf16[64,2,256]{2,1,0:T(2,128)(2,1)S(1)}, u32[]{:S(2)}, u32[]{:S(2)}) async-start(bf16[64,2,256]{2,1,0:T(2,128)(2,1)} %reshape.182), calls=%async_computation.1 | async-start | bytes 131072 | tf_op jit(solution)/shard_map/all_to_all | solution.py:19
  30.6 0.0 copy-start.1
  30.6 1.2 %reduce.6 = s32[64]{0:T(128)S(1)} reduce(s32[64,1,1]{2,1,0:T(1,128)S(1)} %all-to-all-done, s32[]{:T(128)} %constant.6.clone.1), dimensions={1,2}, to_apply=%all_to_all.22.reduce_sub_computation | reduce | bytes 516 | tf_op jit(solution)/shard_map/all_to_all | solution.py:19
  31.8 0.0 copy-done.3
  31.8 0.1 compare_and_fusion
  31.9 8.8 %all-to-all-done.1 = bf16[64,2,256]{2,1,0:T(2,128)(2,1)S(1)} async-done(((bf16[64,2,256]{2,1,0:T(2,128)(2,1)}), bf16[64,2,256]{2,1,0:T(2,128)(2,1)S(1)}, u32[]{:S(2)}, u32[]{:S(2)}) %all-to-all-start.1) | async-done | bytes 65568 | tf_op jit(solution)/shard_map/all_to_all | solution.py:19
  40.7 0.1 reshape.183
  40.7 0.2 convolution_convert_fusion
  41.0 0.0 copy-done
  41.0 0.7 fusion.21
  41.7 0.1 copy.22
  41.8 0.1 select_reduce_fusion
  41.9 0.8 reshape.184
  42.7 4.4 %all-to-all-start.2 = ((f32[64,1,256]{2,1,0:T(1,128)}), f32[64,1,256]{2,1,0:T(1,128)S(1)}, u32[]{:S(2)}, u32[]{:S(2)}) async-start(f32[64,1,256]{2,1,0:T(1,128)} %reshape.184), calls=%async_computation.2 | async-start | bytes 131072 | tf_op jit(solution)/shard_map/all_to_all | solution.py:19
  47.1 0.0 copy-done.1
  47.1 0.4 fusion.11
  47.6 0.2 fusion.9
  47.8 0.1 copy.25
  47.8 0.1 multiply_reduce_fusion
  48.0 9.3 %all-to-all-done.2 = f32[64,1,256]{2,1,0:T(1,128)S(1)} async-done(((f32[64,1,256]{2,1,0:T(1,128)}), f32[64,1,256]{2,1,0:T(1,128)S(1)}, u32[]{:S(2)}, u32[]{:S(2)}) %all-to-all-start.2) | async-done | bytes 65568 | tf_op jit(solution)/shard_map/all_to_all | solution.py:19
  57.2 0.6 broadcast.78
  57.8 0.8 reduce.15
  58.7 0.1 reshape.185
  58.8 0.1 bitcast_reduce_fusion
  58.9 0.5 fusion.1
  59.4 0.1 copy.26
  59.5 0.2 copy.27
  59.7 15.4 %all_to_all.36 = f32[64,1,516]{2,1,0:T(1,128)S(1)} all-to-all(f32[64,1,516]{2,1,0:T(1,128)S(1)} %copy.27), channel_id=1, replica_groups=mesh['inst'=64,'tp'=8] {'inst'}, dimensions={0} | all-to-all | bytes 264192 | tf_op jit(solution)/shard_map/all_to_all | solution.py:45
  75.1 0.1 reduce_sum.40
  75.2 0.1 div.14
  75.3 0.1 broadcast_in_dim.91
  75.4 1.0 reduce.16
  76.5 14.0 %all_to_all.37 = bf16[64,2,256]{2,1,0:T(2,128)(2,1)S(1)} all-to-all(bf16[64,2,256]{2,1,0:T(2,128)(2,1)S(1)} %reshape.186), channel_id=1, replica_groups=mesh['inst'=64,'tp'=8] {'inst'}, dimensions={0} | all-to-all | bytes 131072 | tf_op jit(solution)/shard_map/all_to_all | solution.py:19
  90.5 0.0 copy-start.2
  90.5 0.1 reshape.187
  90.5 0.8 copy-done.2
  91.3 0.1 fusion.3
  92.3 13.1 %all_to_all.38 = f32[64,1,64]{2,1,0:T(1,128)S(1)} all-to-all(f32[64,1,64]{2,1,0:T(1,128)S(1)} %constant_dynamic-update-slice_fusion), channel_id=1, replica_groups=mesh['inst'=64,'tp'=8] {'inst'}, dimensions={0} | all-to-all | bytes 32768 | tf_op jit(solution)/shard_map/all_to_all | solution.py:13
  105.4 0.5 broadcast.76
  105.9 0.7 reduce.13
  106.7 0.1 transpose_reshape_reshape.4
  106.8 13.2 %all_to_all.39 = f32[8,1,512]{2,1,0:T(1,128)S(1)} all-to-all(f32[8,1,512]{2,1,0:T(1,128)S(1)} %transpose_reshape_reshape.4), channel_id=1, replica_groups=mesh['inst'=64,'tp'=8] {'tp'}, dimensions={0} | all-to-all | bytes 32768 | tf_op jit(solution)/shard_map/all_to_all | solution.py:45
  120.0 0.6 convert_element_type.31
  (76 shorter events, 0.8 us)
Async XLA Ops:
  0.0 41.0 %copy-start = (bf16[32,128,128]{2,1,0:T(8,128)(2,1)S(1)}, bf16[32,128,128]{2,1,0:T(8,128)(2,1)}, u32[]{:S(2)}) copy-start(bf16[32,128,128]{2,1,0:T(8,128)(2,1)} %param.9) | copy-start | bytes 3145732
  1.4 15.0 %copy-start.5 = (s32[32]{0:T(128)S(1)}, s32[32]{0:T(128)}, u32[]{:S(2)}) copy-start(s32[32]{0:T(128)} %param.12) | copy-start | bytes 388
  1.4 24.4 %all-to-all-start = ((s32[64,1,1]{2,1,0:T(1,128)}), s32[64,1,1]{2,1,0:T(1,128)S(1)}, u32[]{:S(2)}, u32[]{:S(2)}) async-start(s32[64,1,1]{2,1,0:T(1,128)} %broadcast_in_dim.82), calls=%async_computation | async-start | bytes 65536 | tf_op jit(solution)/shard_map/all_to_all | solution.py:19
  16.3 0.7 copy-start.4
  25.7 6.1 %copy-start.3 = (s32[32]{0:T(128)S(1)}, s32[32]{0:T(128)}, u32[]{:S(2)}) copy-start(s32[32]{0:T(128)} %param.11) | copy-start | bytes 388
  25.7 15.0 %all-to-all-start.1 = ((bf16[64,2,256]{2,1,0:T(2,128)(2,1)}), bf16[64,2,256]{2,1,0:T(2,128)(2,1)S(1)}, u32[]{:S(2)}, u32[]{:S(2)}) async-start(bf16[64,2,256]{2,1,0:T(2,128)(2,1)} %reshape.182), calls=%async_computation.1 | async-start | bytes 131072 | tf_op jit(solution)/shard_map/all_to_all | solution.py:19
  30.6 16.5 %copy-start.1 = (bf16[32,128,128]{2,1,0:T(8,128)(2,1)S(1)}, bf16[32,128,128]{2,1,0:T(8,128)(2,1)}, u32[]{:S(2)}) copy-start(bf16[32,128,128]{2,1,0:T(8,128)(2,1)} %param.10) | copy-start | bytes 3145732
  42.7 14.6 %all-to-all-start.2 = ((f32[64,1,256]{2,1,0:T(1,128)}), f32[64,1,256]{2,1,0:T(1,128)S(1)}, u32[]{:S(2)}, u32[]{:S(2)}) async-start(f32[64,1,256]{2,1,0:T(1,128)} %reshape.184), calls=%async_computation.2 | async-start | bytes 131072 | tf_op jit(solution)/shard_map/all_to_all | solution.py:19
  90.5 0.8 copy-start.2
